TPU v7x, 32 devices: a whole 2x2x4 slice. The times are simulated.
32 devices in a mesh: dp: 4 (over x, core), mp: 8 (over z, y).
Axes of the slice: x: 2, y: 2, z: 4, core: 2. Of those that a mesh axis runs over, the one named last changes fastest.
Arguments:
- cotangent: bfloat16 [512, 4608], P(('dp', 'mp')), may hold values from -50 to 50
- mlp_out: bfloat16 [512, 4608], P(('dp', 'mp')), may hold values from -500 to 500
- post_gain: float32 [4608], replicated, may hold values from 0.5 to 1.5
- down_weight: bfloat16 [36864, 4608], P('mp', 'dp'), may hold values from -0.09375 to 0.09375
- gate_pre: bfloat16 [512, 36864], P('dp', 'mp'), may hold values from -6 to 6
- up_pre: bfloat16 [512, 36864], P('dp', 'mp'), may hold values from -6 to 6
Outputs:
- gate_grad: float32 [512, 36864], P('dp', 'mp')
- up_grad: float32 [512, 36864], P('dp', 'mp')
- gain_grad: float32 [4608], replicated
All inputs are finite; a program needn't handle non-finite values.
Results may differ from a plain program's by a relative error of at most 0.0005.
Values may be sent and summed in bfloat16 or wider, within the bound.
A program may use at most 64 MiB of HBM per device.

v0:
```python
import jax
import jax.numpy as jnp
from jax import lax
from jax.sharding import PartitionSpec as P

D = 4608
epsilon = 1e-06


def gelu_tanh(values):
    return jax.nn.gelu(values, approximate=True)


def local(cotangent, mlp_out, post_gain, down_weight, gate_pre, up_pre):
    forward = mlp_out.astype(jnp.float32)
    upstream = cotangent.astype(jnp.float32)
    root_mean = jnp.sqrt(jnp.mean(forward * forward, axis=1, keepdims=True) + epsilon)
    normed = forward / root_mean
    gain_part = jnp.sum(upstream * normed, axis=0)
    scaled = upstream * post_gain[None, :]
    project_sum = jnp.sum(scaled * forward, axis=1, keepdims=True)
    out_grad = scaled / root_mean - forward * project_sum / (D * root_mean**3)
    hid_units = down_weight.shape[0]
    gain_grad = lax.psum(gain_part, ("dp", "mp"))
    pieces = lax.all_to_all(out_grad, "dp", split_axis=1, concat_axis=0, tiled=True)
    weight_local = down_weight.astype(jnp.float32)
    partial_value = jnp.dot(
        lax.all_gather(pieces, "mp", axis=0, tiled=True),
        weight_local.T,
        precision=lax.Precision.HIGHEST,
    )
    dp_count = lax.axis_size("dp")
    mp_count = lax.axis_size("mp")
    row_count = out_grad.shape[0]
    partial_value = partial_value.reshape(mp_count, dp_count * row_count, hid_units)
    summed = lax.psum_scatter(partial_value, "dp", scatter_dimension=1, tiled=True)
    hidden_grad = summed.reshape(mp_count * row_count, hid_units)
    gate_val = gate_pre.astype(jnp.float32)
    up_val = up_pre.astype(jnp.float32)
    act_val, pull_back = jax.vjp(gelu_tanh, gate_val)
    gate_grad = pull_back(hidden_grad * up_val)[0]
    up_grad = hidden_grad * act_val
    return (gate_grad, up_grad, gain_grad)


def solution(mesh):
    return jax.shard_map(
        local,
        mesh=mesh,
        in_specs=(
            P(("dp", "mp"), None),
            P(("dp", "mp"), None),
            P(),
            P("mp", "dp"),
            P("dp", "mp"),
            P("dp", "mp"),
        ),
        out_specs=(P("dp", "mp"), P("dp", "mp"), P()),
        check_vma=False,
    )
```

profile of v0, /device:TPU:0, one launch (start us, length us, event | category | flops | bytes accessed | tf_op | source)
XLA Modules:
  0.0 187.1 jit_solution(5941770654814540855)
XLA Ops:
  7.2 0.0 all-gather.2.cloned.1.call-start
  7.2 1.1 fusion.12
  8.3 1.3 fusion.11
  9.5 1.1 fusion.10
  10.7 10.5 %all_to_all.19 = f32[16,4,1152]{2,0,1:T(8,128)} all-to-all(f32[16,4,1152]{2,0,1:T(8,128)S(1)} %bitcast.17), channel_id=1, replica_groups=mesh['dp'=4,'mp'=8] {'dp'}, dimensions={1} | all-to-all | bytes 589824 | tf_op jit(solution)/shard_map/all_to_all | solution.py:25
  21.2 0.0 all-gather.2.cloned.1.call-update
  21.2 0.0 reduce-scatter.2.cloned.1.call-start
  21.3 52.6 %all-gather.2.cloned.1.call-done = f32[512,1152]{1,0:T(8,128)} async-done(((f32[64,1152]{1,0:T(8,128)}), f32[512,1152]{1,0:T(8,128)}) %all-gather.2.cloned.1.call-update) | async-done | bytes 2359312 | tf_op jit(solution)/shard_map/all_gather | solution.py:28
  73.9 23.4 %fusion.16 = f32[512,4608]{1,0:T(8,128)} fusion(f32[512,1152]{1,0:T(8,128)} %all-gather.2.cloned.1.call-done, bf16[4608,1152]{1,0:T(8,128)(2,1)} %param.9), kind=kOutput, calls=%fused_computation.31 | convolution fusion | flops 32614907904 | bytes 22413312 | tf_op jit(solution)/shard_map/dot_general | solution.py:27
  97.2 0.0 copy-start
  97.2 0.0 copy-start.1
  97.3 0.0 reduce-scatter.2.cloned.1.call-update
  97.3 40.2 %psum.7 = f32[4608]{0:T(1024)} all-reduce(f32[4608]{0:T(1024)S(1)} %get-tuple-element.3), channel_id=1, replica_groups=mesh['dp'=4,'mp'=8] {'dp','mp'}, use_global_device_ids=true, to_apply=%region_4.0 | all-reduce | flops 4608 | bytes 36864 | tf_op jit(solution)/shard_map/psum | solution.py:24
  137.5 37.0 %reduce-scatter.2.cloned.1.call-done = f32[8,16,4608]{2,1,0:T(8,128)} async-done(((f32[8,64,4608]{2,1,0:T(8,128)}), f32[8,16,4608]{2,1,0:T(8,128)}) %reduce-scatter.2.cloned.1.call-update) | async-done | bytes 2359312 | tf_op jit(solution)/shard_map/reduce_scatter | solution.py:36
  174.5 0.0 copy-done
  174.5 0.0 copy-done.1
  174.5 5.8 %fusion.8 = (f32[128,4608]{1,0:T(8,128)}, f32[128,4608]{1,0:T(8,128)}) fusion(bf16[128,4608]{1,0:T(8,128)(2,1)S(1)} %copy-done, f32[8,16,4608]{2,1,0:T(8,128)} %reduce-scatter.2.cloned.1.call-done, bf16[128,4608]{1,0:T(8,128)(2,1)S(1)} %copy-done.1), kind=kLoop, calls=%fused_computation.13 | loop fusion | flops 14155776 | bytes 9437184 | tf_op jit(solution)/shard_map/mul | solution.py:42
  (2 shorter events, 0.0 us)
Async XLA Ops:
  7.2 66.7 %all-gather.2.cloned.1.call-start = ((), (), s32[]{:S(2)}) async-start(), calls=%async_computation.2 | async-start | bytes 2654208 | tf_op jit(solution)/shard_map/all_gather | solution.py:28
  21.2 153.3 %reduce-scatter.2.cloned.1.call-start = ((), (), s32[]{:S(2)}) async-start(), calls=%async_computation.3 | async-start | bytes 11796480 | tf_op jit(solution)/shard_map/reduce_scatter | solution.py:36
  97.2 77.3 %copy-start = (bf16[128,4608]{1,0:T(8,128)(2,1)S(1)}, bf16[128,4608]{1,0:T(8,128)(2,1)}, u32[]{:S(2)}) copy-start(bf16[128,4608]{1,0:T(8,128)(2,1)} %param.10) | copy-start | bytes 3538948
  97.2 77.3 %copy-start.1 = (bf16[128,4608]{1,0:T(8,128)(2,1)S(1)}, bf16[128,4608]{1,0:T(8,128)(2,1)}, u32[]{:S(2)}) copy-start(bf16[128,4608]{1,0:T(8,128)(2,1)} %param.11) | copy-start | bytes 3538948
Sparse Core Ops, SparseCore 0:
  21.3 52.5 all-gather.1
  97.4 77.0 reduce-scatter.1
where the time goes:
time: 187 us
  waiting for transfers between devices  89.7 us (48%)
  blocking collectives  50.7 us (27%)
  matrix products  23.4 us (13%)
  between operations  14.1 us (8%)
  other arithmetic  9.22 us (5%)
    all_gather x1, waiting for transfers between devices, local(): lax.all_gather(pieces, 'mp', axis=0, tiled=True)  52.6 us
    psum x1, blocking collectives, local(): gain_grad = lax.psum(gain_part, ('dp', 'mp'))  40.2 us
    reduce_scatter x1, waiting for transfers between devices, local(): lax.psum_scatter(partial_value, 'dp', scatter_dimension=1, tiled=True)  37 us
    dot_general x1, matrix products, local(): jnp.dot(lax.all_gather(pieces, 'mp', axis=0, tiled=True), weight_local.T,...  23.4 us
    all_to_all x1, blocking collectives, local(): lax.all_to_all(out_grad, 'dp', split_axis=1, concat_axis=0, tiled=True)  10.5 us
    mul x1, other arithmetic, local(): up_grad = hidden_grad * act_val  5.78 us
  transfers between devices with their start and end apart: 2, of which 2 were waited for; matrix products, arithmetic and copies ran while one was open for 0% of the time, Pallas kernels for 0%

commit v1 on v0

--- a/solution.py
+++ b/solution.py
@@ -22,7 +22,10 @@
     out_grad = scaled / root_mean - forward * project_sum / (D * root_mean**3)
     hid_units = down_weight.shape[0]
     gain_grad = lax.psum(gain_part, ("dp", "mp"))
-    pieces = lax.all_to_all(out_grad, "dp", split_axis=1, concat_axis=0, tiled=True)
+    devices = lax.axis_size("dp")
+    parts = jnp.stack(jnp.split(out_grad, devices, axis=1), axis=0)
+    parts = lax.all_to_all(parts, "dp", split_axis=0, concat_axis=0)
+    pieces = jnp.concatenate(parts, axis=0)
     weight_local = down_weight.astype(jnp.float32)
     partial_value = jnp.dot(
         lax.all_gather(pieces, "mp", axis=0, tiled=True),

time: 187 us -> 187 us (level)
  no operation moved by 1% of the time
where the time goes in v1:
time: 187 us
  waiting for transfers between devices  89.7 us (48%)
  blocking collectives  50.7 us (27%)
  matrix products  23.4 us (13%)
  between operations  14.1 us (8%)
  other arithmetic  9.24 us (5%)
    all_gather x1, waiting for transfers between devices, local(): lax.all_gather(pieces, 'mp', axis=0, tiled=True)  52.6 us
    psum x1, blocking collectives, local(): gain_grad = lax.psum(gain_part, ('dp', 'mp'))  40.2 us
    reduce_scatter x1, waiting for transfers between devices, local(): lax.psum_scatter(partial_value, 'dp', scatter_dimension=1, tiled=True)  37 us
    dot_general x1, matrix products, local(): jnp.dot(lax.all_gather(pieces, 'mp', axis=0, tiled=True), weight_local.T,...  23.4 us
    all_to_all x1, blocking collectives, local(): parts = lax.all_to_all(parts, 'dp', split_axis=0, concat_axis=0)  10.5 us
    mul x1, other arithmetic, local(): up_grad = hidden_grad * act_val  5.78 us
  transfers between devices with their start and end apart: 2, of which 2 were waited for; matrix products, arithmetic and copies ran while one was open for 0% of the time, Pallas kernels for 0%

profile of v1, /device:TPU:0, one launch (start us, length us, event | category | flops | bytes accessed | tf_op | source)
XLA Modules:
  0.0 187.2 jit_solution(6773080797404878615)
XLA Ops:
  7.2 0.0 all-gather.2.cloned.1.call-start
  7.2 1.1 fusion.12
  8.3 1.3 fusion.11
  9.5 1.1 fusion.10
  10.7 10.5 %all_to_all.5 = f32[4,16,1152]{2,1,0:T(8,128)} all-to-all(f32[4,16,1152]{2,1,0:T(8,128)S(1)} %pad_maximum_fusion), channel_id=1, replica_groups=mesh['dp'=4,'mp'=8] {'dp'}, dimensions={0} | all-to-all | bytes 589824 | tf_op jit(solution)/shard_map/all_to_all | solution.py:27
  21.2 0.0 all-gather.2.cloned.1.call-update
  21.2 0.0 reduce-scatter.2.cloned.1.call-start
  21.3 52.6 %all-gather.2.cloned.1.call-done = f32[512,1152]{1,0:T(8,128)} async-done(((f32[64,1152]{1,0:T(8,128)}), f32[512,1152]{1,0:T(8,128)}) %all-gather.2.cloned.1.call-update) | async-done | bytes 2359312 | tf_op jit(solution)/shard_map/all_gather | solution.py:31
  73.9 23.4 %fusion.16 = f32[512,4608]{1,0:T(8,128)} fusion(f32[512,1152]{1,0:T(8,128)} %all-gather.2.cloned.1.call-done, bf16[4608,1152]{1,0:T(8,128)(2,1)} %param.9), kind=kOutput, calls=%fused_computation.35 | convolution fusion | flops 32614907904 | bytes 22413312 | tf_op jit(solution)/shard_map/dot_general | solution.py:30
  97.3 0.0 copy-start
  97.3 0.0 copy-start.1
  97.3 0.0 reduce-scatter.2.cloned.1.call-update
  97.3 40.2 %psum.7 = f32[4608]{0:T(1024)} all-reduce(f32[4608]{0:T(1024)S(1)} %get-tuple-element.3), channel_id=1, replica_groups=mesh['dp'=4,'mp'=8] {'dp','mp'}, use_global_device_ids=true, to_apply=%region_4.0 | all-reduce | flops 4608 | bytes 36864 | tf_op jit(solution)/shard_map/psum | solution.py:24
  137.5 37.0 %reduce-scatter.2.cloned.1.call-done = f32[8,16,4608]{2,1,0:T(8,128)} async-done(((f32[8,64,4608]{2,1,0:T(8,128)}), f32[8,16,4608]{2,1,0:T(8,128)}) %reduce-scatter.2.cloned.1.call-update) | async-done | bytes 2359312 | tf_op jit(solution)/shard_map/reduce_scatter | solution.py:39
  174.5 0.0 copy-done
  174.5 0.0 copy-done.1
  174.5 5.8 %fusion.8 = (f32[128,4608]{1,0:T(8,128)}, f32[128,4608]{1,0:T(8,128)}) fusion(bf16[128,4608]{1,0:T(8,128)(2,1)S(1)} %copy-done, f32[8,16,4608]{2,1,0:T(8,128)} %reduce-scatter.2.cloned.1.call-done, bf16[128,4608]{1,0:T(8,128)(2,1)S(1)} %copy-done.1), kind=kLoop, calls=%fused_computation.13 | loop fusion | flops 14155776 | bytes 9437184 | tf_op jit(solution)/shard_map/mul | solution.py:45
  (3 shorter events, 0.1 us)
Async XLA Ops:
  7.2 66.8 %all-gather.2.cloned.1.call-start = ((), (), s32[]{:S(2)}) async-start(), calls=%async_computation.2 | async-start | bytes 2654208 | tf_op jit(solution)/shard_map/all_gather | solution.py:31
  21.2 153.3 %reduce-scatter.2.cloned.1.call-start = ((), (), s32[]{:S(2)}) async-start(), calls=%async_computation.3 | async-start | bytes 11796480 | tf_op jit(solution)/shard_map/reduce_scatter | solution.py:39
  97.3 77.3 %copy-start = (bf16[128,4608]{1,0:T(8,128)(2,1)S(1)}, bf16[128,4608]{1,0:T(8,128)(2,1)}, u32[]{:S(2)}) copy-start(bf16[128,4608]{1,0:T(8,128)(2,1)} %param.10) | copy-start | bytes 3538948
  97.3 77.3 %copy-start.1 = (bf16[128,4608]{1,0:T(8,128)(2,1)S(1)}, bf16[128,4608]{1,0:T(8,128)(2,1)}, u32[]{:S(2)}) copy-start(bf16[128,4608]{1,0:T(8,128)(2,1)} %param.11) | copy-start | bytes 3538948
Sparse Core Ops, SparseCore 0:
  21.4 52.5 all-gather.1
  97.4 77.0 reduce-scatter.1
